TPU v7x, 32 devices: a whole 2x2x4 slice. The times are simulated.
32 devices in a mesh: paths: 4 (over x, core), cpty: 8 (over z, y).
Axes of the slice: x: 2, y: 2, z: 4, core: 2. Of those that a mesh axis runs over, the one named last changes fastest.
Arguments:
- factors: bfloat16 [64, 6144], P(None, 'paths'), may hold values from -6 to 6
- loadings: bfloat16 [64, 16384], P(None, 'cpty'), may hold values from -2 to 2
- notional: bfloat16 [16384], P('cpty'), may hold values from 0.25 to 0.796875
- strike: bfloat16 [16384], P('cpty'), may hold values from 2 to 8
- curvature: bfloat16 [16384], P('cpty'), may hold values from 1 to 3
- trade_cpty: int32 [16384], P('cpty'), may hold values from 0 to 1023, as said below
Outputs:
- exposure: bfloat16 [6144, 1024], P('paths', 'cpty')
- moment: float32 [1024, 1024], P('paths', 'cpty')
Inputs may be any that keep to these rules, and one draw needn't show every extreme that they name: `trade_cpty`: of the trades in the book of one index of cpty, at most 512 belong to the counterparties numbered k * 128 to (k + 1) * 128 - 1 for any k; in every draw some such k receives exactly 512 from every book.
All inputs are finite; a program needn't handle non-finite values.
Results may differ from a plain program's by a relative error of at most 0.0064.
Values may be sent and summed in bfloat16 or wider, within the bound.
No kernel may reach another device: no remote copies, remote signals or barrier semaphores. Data moves between devices by JAX's collectives and lax.ppermute only.
A program may use at most 128 MiB of HBM per device.

v0:
```python
import jax
import jax.numpy as jnp
from jax import lax
from jax.sharding import PartitionSpec as P

CP_DEV = 128


def price_trades(drivers, loading_cols, trade_terms):
    linear = jnp.dot(drivers, loading_cols, preferred_element_type=jnp.float32)
    terms_wide = trade_terms.astype(jnp.float32)
    value = terms_wide[0] * (linear + terms_wide[2] * jnp.tanh(linear - terms_wide[1]))
    return value.astype(jnp.bfloat16)


def on_device(factors, loadings, notional, strike, curvature, trade_cpty):
    groups = lax.axis_size("cpty")
    own_index = lax.axis_index("cpty")
    trades = loadings.shape[1]
    slot_size = 2 * trades // groups
    owners = trade_cpty // CP_DEV
    marked = (owners[:, None] == jnp.arange(groups, dtype=jnp.int32)[None, :]).astype(jnp.int32)
    ranking = jnp.sum((jnp.cumsum(marked, axis=0) - marked) * marked, axis=1)
    target = owners * slot_size + ranking
    chosen = (
        jnp.zeros((groups * slot_size,), jnp.int32)
        .at[target]
        .set(jnp.arange(trades, dtype=jnp.int32))
    )
    filled = jnp.zeros((groups * slot_size,), jnp.bool_).at[target].set(True)
    labels = jnp.where(filled, trade_cpty[chosen], -1)[None, :]
    drivers = jnp.transpose(factors)
    trade_terms = jnp.stack([notional, strike, curvature])
    described = jnp.concatenate([loadings, trade_terms], axis=0)
    packed = jnp.where(
        filled[None, :], jnp.take(described, chosen, axis=1), jnp.zeros((), jnp.bfloat16)
    )
    received, arrived_ids = (
        lax.all_to_all(packed, "cpty", split_axis=1, concat_axis=1, tiled=True),
        lax.all_to_all(labels, "cpty", split_axis=1, concat_axis=1, tiled=True),
    )
    factor_count = loadings.shape[0]
    arrived = price_trades(drivers, received[:factor_count], received[factor_count:])
    local_ids = arrived_ids[0] - own_index * CP_DEV
    onehot = (local_ids[:, None] == jnp.arange(CP_DEV, dtype=jnp.int32)[None, :]).astype(
        jnp.bfloat16
    )
    netted = jnp.dot(arrived, onehot, preferred_element_type=jnp.float32)
    exposure = jnp.maximum(netted, 0.0).astype(jnp.bfloat16)
    everyone = lax.all_gather(exposure, "cpty", axis=1, tiled=True)
    path_total = exposure.shape[0] * lax.axis_size("paths")
    moment = (
        lax.psum_scatter(
            jnp.einsum("pa,pb->ab", everyone, exposure, preferred_element_type=jnp.float32),
            "paths",
            scatter_dimension=0,
            tiled=True,
        )
        / path_total
    )
    return (exposure, moment)


def solution(mesh):
    in_specs = (P(None, "paths"), P(None, "cpty"), P("cpty"), P("cpty"), P("cpty"), P("cpty"))
    out_specs = (P("paths", "cpty"), P("paths", "cpty"))
    return jax.shard_map(
        on_device, mesh=mesh, in_specs=in_specs, out_specs=out_specs, check_vma=False
    )
```

profile of v0, /device:TPU:0, one launch (start us, length us, event | category | flops | bytes accessed | tf_op | source)
XLA Modules:
  0.0 204.9 jit_solution(14715116246756037690)
XLA Ops:
  7.2 0.0 copy-start
  7.2 0.0 copy-start.1
  7.2 0.8 add_select_fusion
  8.0 2.3 %reduce-window.6 = s32[8,16,128]{2,1,0:T(8,128)S(1)} reduce-window(s32[8,16,128]{2,1,0:T(8,128)S(1)} %fusion.14, s32[]{:T(128)} %constant.24.clone.1), window={size=1x1x128 pad=0_0x0_0x127_0}, to_apply=%region_0.1 | reduce-window | flops 2080768 | bytes 131076 | tf_op jit(solution)/shard_map/reduce-window
  10.3 0.3 slice_reduce_fusion
  10.5 0.2 reduce-window.9
  10.7 0.1 add_bitcast_fusion
  10.9 0.7 compare_select_fusion.1
  11.6 8.1 %scatter_custom_fusion.1 = s32[4096]{0:T(1024)S(1)} fusion(s32[2048]{0:T(1024)S(1)} %compare_select_fusion.1, s32[2048]{0:T(1024)S(1)} %iota.15, s32[]{:T(128)} %constant.24.clone.1), kind=kCustom, calls=%fused_computation.43 | custom fusion | bytes 16388 | tf_op jit(solution)/shard_map/scatter | solution.py:28
  19.7 0.0 copy-done.1
  19.7 0.0 copy-start.2
  19.7 0.0 copy-start.3
  19.7 0.0 copy-start.4
  19.7 0.0 copy-start.5
  19.7 23.0 %gather_fusion.1 = s32[4096]{0:T(1024)S(1)} fusion(s32[2048]{0:T(1024)S(1)} %copy-done.1, s32[4096]{0:T(1024)S(1)} %fusion.15), kind=kCustom, calls=%fused_computation.1 | custom fusion | bytes 49152 | tf_op jit(solution)/shard_map/gather | solution.py:31
  42.8 9.1 %scatter_custom_fusion = pred[4096]{0:T(1024)(128)(4,1)S(1)} fusion(s32[2048]{0:T(1024)S(1)} %compare_select_fusion.1, pred[2048]{0:T(1024)(128)(4,1)S(1)} %broadcast.49, pred[]{:T(512)} %constant.22.clone.1), kind=kCustom, calls=%fused_computation.47 | custom fusion | bytes 4097 | tf_op jit(solution)/shard_map/scatter | solution.py:30
  51.9 0.6 broadcast_select_fusion
  52.5 7.3 %all-to-all-start.1 = ((s32[1,8,512]{2,0,1:T(1,128)}), s32[1,8,512]{2,0,1:T(1,128)S(1)}, u32[]{:S(2)}, u32[]{:S(2)}) async-start(s32[1,8,512]{2,0,1:T(1,128)} %bitcast.8), calls=%async_computation.1 | async-start | bytes 32768 | tf_op jit(solution)/shard_map/all_to_all | solution.py:40
  59.9 0.0 copy-done.2
  59.9 0.3 copy.19
  60.2 0.0 copy-done.3
  60.2 0.3 stack.12
  60.5 0.0 copy-done.4
  60.5 0.3 stack.13
  60.9 0.0 copy-done.5
  60.9 0.3 stack.14
  61.2 0.7 pad_maximum_fusion
  61.9 12.1 %gather_fusion = bf16[4096,67]{1,0:T(8,128)(2,1)S(1)} fusion(bf16[67,2048]{0,1:T(8,128)(2,1)S(1)} %pad_maximum_fusion, s32[4096]{0:T(1024)S(1)} %fusion.15), kind=kCustom, calls=%fused_computation | custom fusion | bytes 1114112 | tf_op jit(solution)/shard_map/jit(_take)/gather | solution.py:36
  74.1 0.6 copy.23
  74.6 0.9 select_select_fusion
  75.5 0.0 all-to-all-done.1
  75.5 6.0 %all-to-all-start = ((bf16[67,8,512]{2,0,1:T(8,128)(2,1)}), bf16[67,8,512]{2,0,1:T(8,128)(2,1)S(1)}, u32[]{:S(2)}, u32[]{:S(2)}) async-start(bf16[67,8,512]{2,0,1:T(8,128)(2,1)} %select_select_fusion), calls=%async_computation | async-start | bytes 1179648 | tf_op jit(solution)/shard_map/all_to_all | solution.py:39
  81.5 0.0 all-gather.2.cloned.1.call-start
  81.6 0.9 iota_compare_fusion.7
  82.5 14.4 %all-to-all-done = bf16[67,8,512]{2,0,1:T(8,128)(2,1)S(1)} async-done(((bf16[67,8,512]{2,0,1:T(8,128)(2,1)}), bf16[67,8,512]{2,0,1:T(8,128)(2,1)S(1)}, u32[]{:S(2)}, u32[]{:S(2)}) %all-to-all-start) | async-done | bytes 548896 | tf_op jit(solution)/shard_map/all_to_all | solution.py:39
  97.1 0.0 copy-done
  97.1 13.8 %fusion.9 = bf16[1536,128]{1,0:T(8,128)(2,1)} fusion(bf16[64,4096]{1,0:T(8,128)(2,1)S(1)} %bitcast.70, bf16[64,1536]{1,0:T(8,128)(2,1)S(1)} %copy-done, f32[4096]{0:T(1024)S(1)} %bitcast.75, f32[4096]{0:T(1024)S(1)} %bitcast.76, f32[4096]{0:T(1024)S(1)} %bitcast.74, pred[4096,128]{1,0:T(32,128)(4,1)S(1)} %iota_compare_fusion.7), kind=kOutput, calls=%fused_computation.15 | convolution fusion | flops 2447769600 | bytes 1687552 | tf_op jit(solution)/shard_map/dot_general | solution.py:48
  110.8 0.0 all-gather.2.cloned.1.call-update
  110.9 0.0 reduce-scatter.2.cloned.1.call-start
  110.9 61.8 %all-gather.2.cloned.1.call-done = bf16[1536,1024]{1,0:T(8,128)(2,1)} async-done(((bf16[1536,128]{1,0:T(8,128)(2,1)}), bf16[1536,1024]{1,0:T(8,128)(2,1)}) %all-gather.2.cloned.1.call-update) | async-done | bytes 3145744 | tf_op jit(solution)/shard_map/all_gather | solution.py:50
  172.7 3.7 %fusion.24 = f32[1024,128]{1,0:T(8,128)} fusion(bf16[1536,1024]{1,0:T(8,128)(2,1)} %all-gather.2.cloned.1.call-done, bf16[1536,128]{1,0:T(8,128)(2,1)} %fusion.9), kind=kOutput, calls=%fused_computation.51 | convolution fusion | flops 402653184 | bytes 4063232 | tf_op jit(solution)/shard_map/pa,pb->ab/dot_general | solution.py:54
  176.5 0.0 reduce-scatter.2.cloned.1.call-update
  176.5 20.0 %reduce-scatter.2.cloned.1.call-done = f32[256,128]{1,0:T(8,128)} async-done(((f32[1024,128]{1,0:T(8,128)}), f32[256,128]{1,0:T(8,128)}) %reduce-scatter.2.cloned.1.call-update) | async-done | bytes 131088 | tf_op jit(solution)/shard_map/reduce_scatter | solution.py:53
  196.4 1.6 broadcast_multiply_fusion
  (13 shorter events, 0.2 us)
Async XLA Ops:
  7.2 89.9 %copy-start = (bf16[64,1536]{1,0:T(8,128)(2,1)S(1)}, bf16[64,1536]{1,0:T(8,128)(2,1)}, u32[]{:S(2)}) copy-start(bf16[64,1536]{1,0:T(8,128)(2,1)} %param.6) | copy-start | bytes 589828
  7.2 12.5 %copy-start.1 = (s32[2048]{0:T(1024)S(1)}, s32[2048]{0:T(1024)}, u32[]{:S(2)}) copy-start(s32[2048]{0:T(1024)} %param.11) | copy-start | bytes 24580
  19.7 40.2 %copy-start.2 = (bf16[64,2048]{1,0:T(8,128)(2,1)S(1)}, bf16[64,2048]{1,0:T(8,128)(2,1)}, u32[]{:S(2)}) copy-start(bf16[64,2048]{1,0:T(8,128)(2,1)} %param.7) | copy-start | bytes 786436
  19.7 40.5 %copy-start.3 = (bf16[2048]{0:T(1024)(128)(2,1)S(1)}, bf16[2048]{0:T(1024)(128)(2,1)}, u32[]{:S(2)}) copy-start(bf16[2048]{0:T(1024)(128)(2,1)} %param.8) | copy-start | bytes 12292
  19.7 40.8 %copy-start.4 = (bf16[2048]{0:T(1024)(128)(2,1)S(1)}, bf16[2048]{0:T(1024)(128)(2,1)}, u32[]{:S(2)}) copy-start(bf16[2048]{0:T(1024)(128)(2,1)} %param.9) | copy-start | bytes 12292
  19.7 41.2 %copy-start.5 = (bf16[2048]{0:T(1024)(128)(2,1)S(1)}, bf16[2048]{0:T(1024)(128)(2,1)}, u32[]{:S(2)}) copy-start(bf16[2048]{0:T(1024)(128)(2,1)} %param.10) | copy-start | bytes 12292
  52.5 23.0 %all-to-all-start.1 = ((s32[1,8,512]{2,0,1:T(1,128)}), s32[1,8,512]{2,0,1:T(1,128)S(1)}, u32[]{:S(2)}, u32[]{:S(2)}) async-start(s32[1,8,512]{2,0,1:T(1,128)} %bitcast.8), calls=%async_computation.1 | async-start | bytes 32768 | tf_op jit(solution)/shard_map/all_to_all | solution.py:40
  75.5 21.4 %all-to-all-start = ((bf16[67,8,512]{2,0,1:T(8,128)(2,1)}), bf16[67,8,512]{2,0,1:T(8,128)(2,1)S(1)}, u32[]{:S(2)}, u32[]{:S(2)}) async-start(bf16[67,8,512]{2,0,1:T(8,128)(2,1)} %select_select_fusion), calls=%async_computation | async-start | bytes 1179648 | tf_op jit(solution)/shard_map/all_to_all | solution.py:39
  81.5 91.2 %all-gather.2.cloned.1.call-start = ((), (), s32[]{:S(2)}) async-start(), calls=%async_computation.3 | async-start | bytes 3538944 | tf_op jit(solution)/shard_map/all_gather | solution.py:50
  110.9 85.6 %reduce-scatter.2.cloned.1.call-start = ((), (), s32[]{:S(2)}) async-start(), calls=%async_computation.4 | async-start | bytes 655360 | tf_op jit(solution)/shard_map/reduce_scatter | solution.py:53
Sparse Core Ops, SparseCore 0:
  111.0 61.6 all-gather.1
  176.6 19.7 reduce-scatter.1
where the time goes:
time: 205 us
  waiting for transfers between devices  96.2 us (47%)
  local copies, waits for them, and re-layouts  54.7 us (27%)
  matrix products  17.5 us (9%)
  between operations  14.3 us (7%)
  starting transfers between devices  13.4 us (7%)
  other arithmetic  8.76 us (4%)
    all_gather x1, waiting for transfers between devices, on_device(): everyone = lax.all_gather(exposure, 'cpty', axis=1, tiled=True)  61.8 us
    gather x1, local copies, waits for them, and re-layouts, on_device(): labels = jnp.where(filled, trade_cpty[chosen], -1)[None, :]  23 us
    reduce_scatter x1, waiting for transfers between devices, on_device(): lax.psum_scatter(jnp.einsum('pa,pb->ab', everyone, exposure, preferred_el...  20 us
    all_to_all x1, waiting for transfers between devices, on_device(): lax.all_to_all(packed, 'cpty', split_axis=1, concat_axis=1, tiled=True)  14.4 us
    dot_general x1, matrix products, on_device(): netted = jnp.dot(arrived, onehot, preferred_element_type=jnp.float32)  13.8 us
    gather x2, local copies, waits for them, and re-layouts, on_device(): jnp.take(described, chosen, axis=1)  12.7 us
    scatter x1, local copies, waits for them, and re-layouts, on_device(): filled = jnp.zeros((groups * slot_size,), jnp.bool_).at[target].set(True)  9.13 us
    scatter x1, local copies, waits for them, and re-layouts, on_device(): chosen = jnp.zeros((groups * slot_size,), jnp.int32).at[target].set(jnp.a...  8.06 us
  transfers between devices with their start and end apart: 4, of which 3 were waited for; matrix products, arithmetic and copies ran while one was open for 8% of the time, Pallas kernels for 0%

commit v1 on v0

--- a/solution.py
+++ b/solution.py
@@ -4,6 +4,10 @@
 from jax.sharding import PartitionSpec as P
 
 CP_DEV = 128
+
+
+def render_frames_up(piece_in, join_dim):
+    return jnp.concatenate(jax.lax.all_gather(piece_in, "cpty"), axis=join_dim)
 
 
 def price_trades(drivers, loading_cols, trade_terms):
@@ -47,7 +51,7 @@
     )
     netted = jnp.dot(arrived, onehot, preferred_element_type=jnp.float32)
     exposure = jnp.maximum(netted, 0.0).astype(jnp.bfloat16)
-    everyone = lax.all_gather(exposure, "cpty", axis=1, tiled=True)
+    everyone = render_frames_up(exposure, 1)
     path_total = exposure.shape[0] * lax.axis_size("paths")
     moment = (
         lax.psum_scatter(

time: 205 us -> 205 us (level)
  local copies, waits for them, and re-layouts: 54.7 us -> 57.9 us
  waiting for transfers between devices: 96.2 us -> 94.1 us
    all_gather x0 -> x1, local copies, waits for them, and re-layouts: none -> 3.18 us  [render_frames_up(): return jnp.concatenate(jax.lax.all_gather(piece_in, 'cpty'), axis=join_dim)]
    all_gather x1, waiting for transfers between devices: 61.8 us -> 59.2 us  [render_frames_up(): return jnp.concatenate(jax.lax.all_gather(piece_in, 'cpty'), axis=join_dim)]
where the time goes in v1:
time: 205 us
  waiting for transfers between devices  94.1 us (46%)
  local copies, waits for them, and re-layouts  57.9 us (28%)
  matrix products  16.5 us (8%)
  between operations  14.3 us (7%)
  starting transfers between devices  13.4 us (7%)
  other arithmetic  8.76 us (4%)
    all_gather x1, waiting for transfers between devices, render_frames_up(): return jnp.concatenate(jax.lax.all_gather(piece_in, 'cpty'), axis=join_dim)  59.2 us
    gather x1, local copies, waits for them, and re-layouts, on_device(): labels = jnp.where(filled, trade_cpty[chosen], -1)[None, :]  23 us
    reduce_scatter x1, waiting for transfers between devices, on_device(): lax.psum_scatter(jnp.einsum('pa,pb->ab', everyone, exposure, preferred_el...  20.5 us
    all_to_all x1, waiting for transfers between devices, on_device(): lax.all_to_all(packed, 'cpty', split_axis=1, concat_axis=1, tiled=True)  14.4 us
    dot_general x1, matrix products, on_device(): netted = jnp.dot(arrived, onehot, preferred_element_type=jnp.float32)  13.8 us
    gather x2, local copies, waits for them, and re-layouts, on_device(): jnp.take(described, chosen, axis=1)  12.7 us
    scatter x1, local copies, waits for them, and re-layouts, on_device(): filled = jnp.zeros((groups * slot_size,), jnp.bool_).at[target].set(True)  9.13 us
    scatter x1, local copies, waits for them, and re-layouts, on_device(): chosen = jnp.zeros((groups * slot_size,), jnp.int32).at[target].set(jnp.a...  8.06 us
  transfers between devices with their start and end apart: 4, of which 3 were waited for; matrix products, arithmetic and copies ran while one was open for 8% of the time, Pallas kernels for 0%

profile of v1, /device:TPU:0, one launch (start us, length us, event | category | flops | bytes accessed | tf_op | source)
XLA Modules:
  0.0 205.0 jit_solution(950302255255442821)
XLA Ops:
  7.2 0.0 copy-start
  7.2 0.0 copy-start.1
  7.2 0.8 add_select_fusion
  8.0 2.3 %reduce-window.6 = s32[8,16,128]{2,1,0:T(8,128)S(1)} reduce-window(s32[8,16,128]{2,1,0:T(8,128)S(1)} %fusion.14, s32[]{:T(128)} %constant.24.clone.1), window={size=1x1x128 pad=0_0x0_0x127_0}, to_apply=%region_0.1 | reduce-window | flops 2080768 | bytes 131076 | tf_op jit(solution)/shard_map/reduce-window
  10.3 0.3 slice_reduce_fusion
  10.5 0.2 reduce-window.9
  10.7 0.1 add_bitcast_fusion
  10.9 0.7 compare_select_fusion.1
  11.6 8.1 %scatter_custom_fusion.1 = s32[4096]{0:T(1024)S(1)} fusion(s32[2048]{0:T(1024)S(1)} %compare_select_fusion.1, s32[2048]{0:T(1024)S(1)} %iota.15, s32[]{:T(128)} %constant.24.clone.1), kind=kCustom, calls=%fused_computation.43 | custom fusion | bytes 16388 | tf_op jit(solution)/shard_map/scatter | solution.py:32
  19.7 0.0 copy-done.1
  19.7 0.0 copy-start.2
  19.7 0.0 copy-start.3
  19.7 0.0 copy-start.4
  19.7 0.0 copy-start.5
  19.7 23.0 %gather_fusion.1 = s32[4096]{0:T(1024)S(1)} fusion(s32[2048]{0:T(1024)S(1)} %copy-done.1, s32[4096]{0:T(1024)S(1)} %fusion.15), kind=kCustom, calls=%fused_computation.1 | custom fusion | bytes 49152 | tf_op jit(solution)/shard_map/gather | solution.py:35
  42.8 9.1 %scatter_custom_fusion = pred[4096]{0:T(1024)(128)(4,1)S(1)} fusion(s32[2048]{0:T(1024)S(1)} %compare_select_fusion.1, pred[2048]{0:T(1024)(128)(4,1)S(1)} %broadcast.49, pred[]{:T(512)} %constant.22.clone.1), kind=kCustom, calls=%fused_computation.47 | custom fusion | bytes 4097 | tf_op jit(solution)/shard_map/scatter | solution.py:34
  51.9 0.6 broadcast_select_fusion
  52.5 7.3 %all-to-all-start.1 = ((s32[1,8,512]{2,0,1:T(1,128)}), s32[1,8,512]{2,0,1:T(1,128)S(1)}, u32[]{:S(2)}, u32[]{:S(2)}) async-start(s32[1,8,512]{2,0,1:T(1,128)} %bitcast.8), calls=%async_computation.1 | async-start | bytes 32768 | tf_op jit(solution)/shard_map/all_to_all | solution.py:44
  59.9 0.0 copy-done.2
  59.9 0.3 copy.21
  60.2 0.0 copy-done.3
  60.2 0.3 stack.12
  60.5 0.0 copy-done.4
  60.5 0.3 stack.13
  60.9 0.0 copy-done.5
  60.9 0.3 stack.14
  61.2 0.7 pad_maximum_fusion
  61.9 12.1 %gather_fusion = bf16[4096,67]{1,0:T(8,128)(2,1)S(1)} fusion(bf16[67,2048]{0,1:T(8,128)(2,1)S(1)} %pad_maximum_fusion, s32[4096]{0:T(1024)S(1)} %fusion.15), kind=kCustom, calls=%fused_computation | custom fusion | bytes 1114112 | tf_op jit(solution)/shard_map/jit(_take)/gather | solution.py:40
  74.1 0.6 copy.25
  74.6 0.9 select_select_fusion
  75.5 0.0 all-to-all-done.1
  75.5 6.0 %all-to-all-start = ((bf16[67,8,512]{2,0,1:T(8,128)(2,1)}), bf16[67,8,512]{2,0,1:T(8,128)(2,1)S(1)}, u32[]{:S(2)}, u32[]{:S(2)}) async-start(bf16[67,8,512]{2,0,1:T(8,128)(2,1)} %select_select_fusion), calls=%async_computation | async-start | bytes 1179648 | tf_op jit(solution)/shard_map/all_to_all | solution.py:43
  81.5 0.0 all-gather.3.cloned.1.call-start
  81.6 0.9 iota_compare_fusion.7
  82.5 14.4 %all-to-all-done = bf16[67,8,512]{2,0,1:T(8,128)(2,1)S(1)} async-done(((bf16[67,8,512]{2,0,1:T(8,128)(2,1)}), bf16[67,8,512]{2,0,1:T(8,128)(2,1)S(1)}, u32[]{:S(2)}, u32[]{:S(2)}) %all-to-all-start) | async-done | bytes 548896 | tf_op jit(solution)/shard_map/all_to_all | solution.py:43
  97.1 0.0 copy-done
  97.1 13.8 %fusion.9 = bf16[1536,128]{1,0:T(8,128)(2,1)} fusion(bf16[64,4096]{1,0:T(8,128)(2,1)S(1)} %bitcast.76, bf16[64,1536]{1,0:T(8,128)(2,1)S(1)} %copy-done, f32[4096]{0:T(1024)S(1)} %bitcast.81, f32[4096]{0:T(1024)S(1)} %bitcast.82, f32[4096]{0:T(1024)S(1)} %bitcast.80, pred[4096,128]{1,0:T(32,128)(4,1)S(1)} %iota_compare_fusion.7), kind=kOutput, calls=%fused_computation.15 | convolution fusion | flops 2447769600 | bytes 1687552 | tf_op jit(solution)/shard_map/dot_general | solution.py:52
  110.8 0.0 all-gather.3.cloned.1.call-update
  110.9 0.0 reduce-scatter.2.cloned.1.call-start
  110.9 59.2 %all-gather.3.cloned.1.call-done = bf16[12288,128]{1,0:T(8,128)(2,1)} async-done(((bf16[1536,128]{1,0:T(8,128)(2,1)}), bf16[12288,128]{1,0:T(8,128)(2,1)}) %all-gather.3.cloned.1.call-update) | async-done | bytes 3145744 | tf_op jit(solution)/shard_map/all_gather | solution.py:10
  170.1 3.2 %copy.27 = bf16[8,1536,128]{1,2,0:T(8,128)(2,1)S(1)} copy(bf16[8,1536,128]{2,1,0:T(8,128)(2,1)} %bitcast.74) | data formatting | bytes 6291456 | tf_op jit(solution)/shard_map/all_gather | solution.py:10
  173.3 2.8 %fusion.24 = f32[1024,128]{1,0:T(8,128)} fusion(bf16[1536,1024]{0,1:T(8,128)(2,1)S(1)} %bitcast.73, bf16[1536,128]{1,0:T(8,128)(2,1)} %fusion.9), kind=kOutput, calls=%fused_computation.51 | convolution fusion | flops 402653184 | bytes 4063232 | tf_op jit(solution)/shard_map/pa,pb->ab/dot_general | solution.py:58
  176.0 0.0 reduce-scatter.2.cloned.1.call-update
  176.1 20.5 %reduce-scatter.2.cloned.1.call-done = f32[256,128]{1,0:T(8,128)} async-done(((f32[1024,128]{1,0:T(8,128)}), f32[256,128]{1,0:T(8,128)}) %reduce-scatter.2.cloned.1.call-update) | async-done | bytes 131088 | tf_op jit(solution)/shard_map/reduce_scatter | solution.py:57
  196.6 1.6 broadcast_multiply_fusion
  (13 shorter events, 0.2 us)
Async XLA Ops:
  7.2 89.9 %copy-start = (bf16[64,1536]{1,0:T(8,128)(2,1)S(1)}, bf16[64,1536]{1,0:T(8,128)(2,1)}, u32[]{:S(2)}) copy-start(bf16[64,1536]{1,0:T(8,128)(2,1)} %param.6) | copy-start | bytes 589828
  7.2 12.5 %copy-start.1 = (s32[2048]{0:T(1024)S(1)}, s32[2048]{0:T(1024)}, u32[]{:S(2)}) copy-start(s32[2048]{0:T(1024)} %param.11) | copy-start | bytes 24580
  19.7 40.2 %copy-start.2 = (bf16[64,2048]{1,0:T(8,128)(2,1)S(1)}, bf16[64,2048]{1,0:T(8,128)(2,1)}, u32[]{:S(2)}) copy-start(bf16[64,2048]{1,0:T(8,128)(2,1)} %param.7) | copy-start | bytes 786436
  19.7 40.5 %copy-start.3 = (bf16[2048]{0:T(1024)(128)(2,1)S(1)}, bf16[2048]{0:T(1024)(128)(2,1)}, u32[]{:S(2)}) copy-start(bf16[2048]{0:T(1024)(128)(2,1)} %param.8) | copy-start | bytes 12292
  19.7 40.8 %copy-start.4 = (bf16[2048]{0:T(1024)(128)(2,1)S(1)}, bf16[2048]{0:T(1024)(128)(2,1)}, u32[]{:S(2)}) copy-start(bf16[2048]{0:T(1024)(128)(2,1)} %param.9) | copy-start | bytes 12292
  19.7 41.2 %copy-start.5 = (bf16[2048]{0:T(1024)(128)(2,1)S(1)}, bf16[2048]{0:T(1024)(128)(2,1)}, u32[]{:S(2)}) copy-start(bf16[2048]{0:T(1024)(128)(2,1)} %param.10) | copy-start | bytes 12292
  52.5 23.0 %all-to-all-start.1 = ((s32[1,8,512]{2,0,1:T(1,128)}), s32[1,8,512]{2,0,1:T(1,128)S(1)}, u32[]{:S(2)}, u32[]{:S(2)}) async-start(s32[1,8,512]{2,0,1:T(1,128)} %bitcast.8), calls=%async_computation.1 | async-start | bytes 32768 | tf_op jit(solution)/shard_map/all_to_all | solution.py:44
  75.5 21.4 %all-to-all-start = ((bf16[67,8,512]{2,0,1:T(8,128)(2,1)}), bf16[67,8,512]{2,0,1:T(8,128)(2,1)S(1)}, u32[]{:S(2)}, u32[]{:S(2)}) async-start(bf16[67,8,512]{2,0,1:T(8,128)(2,1)} %select_select_fusion), calls=%async_computation | async-start | bytes 1179648 | tf_op jit(solution)/shard_map/all_to_all | solution.py:43
  81.5 88.5 %all-gather.3.cloned.1.call-start = ((), (), s32[]{:S(2)}) async-start(), calls=%async_computation.4 | async-start | bytes 3538944 | tf_op jit(solution)/shard_map/all_gather | solution.py:10
  110.9 85.7 %reduce-scatter.2.cloned.1.call-start = ((), (), s32[]{:S(2)}) async-start(), calls=%async_computation.3 | async-start | bytes 655360 | tf_op jit(solution)/shard_map/reduce_scatter | solution.py:57
Sparse Core Ops, SparseCore 0:
  111.0 59.0 all-gather.2
  176.2 20.3 reduce-scatter.1
